TPU v7x, 32 devices: a whole 2x2x4 slice. The times are simulated.
32 devices in a mesh: dp: 8 (over y, x, core), tensor: 4 (over z).
Axes of the slice: x: 2, y: 2, z: 4, core: 2. Of those that a mesh axis runs over, the one named last changes fastest.
Arguments:
- tokens: bfloat16 [128, 196, 768], P(('dp', 'tensor')), may hold values from -6 to 6
- space_gain: float32 [768], replicated, may hold values from 0.5 to 1.5
- space_shift: float32 [768], replicated, may hold values from -3 to 3
- space_inproj: bfloat16 [768, 3, 768], P(None, None, 'tensor'), may hold values from -0.21875 to 0.21875
- space_bias: bfloat16 [2, 768], P(None, 'tensor'), may hold values from -3 to 3
- space_outproj: bfloat16 [768, 768], P('tensor'), may hold values from -1.75 to 1.75
- space_outbias: bfloat16 [768], replicated, may hold values from -3 to 3
- time_gain: float32 [768], replicated, may hold values from 0.5 to 1.5
- time_shift: float32 [768], replicated, may hold values from -3 to 3
- time_inproj: bfloat16 [768, 3, 768], P(None, None, 'tensor'), may hold values from -0.21875 to 0.21875
- time_bias: bfloat16 [2, 768], P(None, 'tensor'), may hold values from -3 to 3
- time_outproj: bfloat16 [768, 768], P('tensor'), may hold values from -0.5 to 0.5
- time_outbias: bfloat16 [768], replicated, may hold values from -3 to 3
- feed_gain: float32 [768], replicated, may hold values from 0.5 to 1.5
- feed_shift: float32 [768], replicated, may hold values from -3 to 3
- up_weight: bfloat16 [3072, 768], P('tensor'), may hold values from -0.21875 to 0.21875
- up_bias: bfloat16 [3072], P('tensor'), may hold values from -3 to 3
- down_weight: bfloat16 [3072, 768], P('tensor'), may hold values from -0.15625 to 0.15625
- down_bias: bfloat16 [768], replicated, may hold values from -3 to 3
- cotangent: bfloat16 [128, 196, 768], P(('dp', 'tensor')), may hold values from -6 to 6
Outputs:
- layer_out: bfloat16 [128, 196, 768], P(('dp', 'tensor'))
- input_gradient: float32 [128, 196, 768], P(('dp', 'tensor'))
- space_gain_gradient: float32 [768], replicated
- space_shift_gradient: float32 [768], replicated
- space_inproj_gradient: float32 [768, 3, 768], P(None, None, 'tensor')
- space_bias_gradient: float32 [2, 768], P(None, 'tensor')
- space_outproj_gradient: float32 [768, 768], P('tensor')
- space_outbias_gradient: float32 [768], replicated
- time_gain_gradient: float32 [768], replicated
- time_shift_gradient: float32 [768], replicated
- time_inproj_gradient: float32 [768, 3, 768], P(None, None, 'tensor')
- time_bias_gradient: float32 [2, 768], P(None, 'tensor')
- time_outproj_gradient: float32 [768, 768], P('tensor')
- time_outbias_gradient: float32 [768], replicated
- feed_gain_gradient: float32 [768], replicated
- feed_shift_gradient: float32 [768], replicated
- up_weight_gradient: float32 [3072, 768], P('tensor')
- up_bias_gradient: float32 [3072], P('tensor')
- down_weight_gradient: float32 [3072, 768], P('tensor')
- down_bias_gradient: float32 [768], replicated
All inputs are finite; a program needn't handle non-finite values.
Results may differ from a plain program's by a relative error of at most 0.013.
The roundings to bfloat16 on the way count: a program that leaves them out, or rounds other values in their place, can miss the bound.
Values may be sent and summed in bfloat16 or wider, within the bound.
A program may use at most 192 MiB of HBM per device.

v0:
```python
import jax
import jax.numpy as jnp
from jax import lax
from jax.sharding import PartitionSpec as P

HS = 64
PATCH = 196
TIMES = 16
EPSILON = 1e-06
ROOT_HALF = 0.7071067811865476
INV_ROOT_TAU = 0.3989422804014327


def layer_norm(values, gain, shift):
    center = values - jnp.mean(values, axis=-1, keepdims=True)
    second = jnp.mean(center * center, axis=-1, keepdims=True)
    return center * lax.rsqrt(second + EPSILON) * gain + shift


def gelu_exact(values):
    return 0.5 * values * (1.0 + lax.erf(values * ROOT_HALF))


def gelu_slope(values):
    return (
        0.5 * (1.0 + lax.erf(values * ROOT_HALF))
        + values * jnp.exp(-0.5 * values * values) * INV_ROOT_TAU
    )


def head_forms(batch_first):
    if batch_first:
        return ("blhe", "bmhe", "bhlm")
    return ("lbhe", "mbhe", "bhlm")


def attend(queries, keys, values, batch_first):
    query_form, key_form, score_form = head_forms(batch_first)
    qk_scale = HS ** (-0.5)
    scores = (
        jnp.einsum(
            query_form + "," + key_form + "->" + score_form,
            queries,
            keys,
            preferred_element_type=jnp.float32,
        )
        * qk_scale
    )
    top = jnp.max(scores, axis=-1, keepdims=True)
    weights = jnp.exp(scores - top)
    total = jnp.sum(weights, axis=-1, keepdims=True)
    probs = (weights / total).astype(jnp.bfloat16)
    mixed = jnp.einsum(
        score_form + "," + key_form + "->" + query_form,
        probs,
        values,
        preferred_element_type=jnp.float32,
    )
    return (mixed, top + jnp.log(total))


def attend_back(queries, keys, values, log_total, mixed_grad, batch_first):
    query_form, key_form, score_form = head_forms(batch_first)
    qk_scale = HS ** (-0.5)
    to_scores = query_form + "," + key_form + "->" + score_form
    scores = jnp.einsum(to_scores, queries, keys, preferred_element_type=jnp.float32) * qk_scale
    probs = jnp.exp(scores - log_total)
    value_grad = jnp.einsum(
        score_form + "," + query_form + "->" + key_form,
        probs.astype(jnp.bfloat16),
        mixed_grad,
        preferred_element_type=jnp.float32,
    )
    prob_grad = jnp.einsum(to_scores, mixed_grad, values, preferred_element_type=jnp.float32)
    inner = jnp.sum(prob_grad * probs, axis=-1, keepdims=True)
    score_grad = (probs * (prob_grad - inner)).astype(jnp.bfloat16)
    query_grad = (
        jnp.einsum(
            score_form + "," + key_form + "->" + query_form,
            score_grad,
            keys,
            preferred_element_type=jnp.float32,
        )
        * qk_scale
    )
    key_grad = (
        jnp.einsum(
            score_form + "," + query_form + "->" + key_form,
            score_grad,
            queries,
            preferred_element_type=jnp.float32,
        )
        * qk_scale
    )
    return (query_grad, key_grad, value_grad)


def full_rows(shard):
    return lax.all_gather(shard, "tensor", axis=0, tiled=True)


def partial_rows(make_term, own_rows):
    return lax.psum_scatter(
        make_term(jnp.int32(0), own_rows * lax.axis_size("tensor")),
        "tensor",
        scatter_dimension=0,
        tiled=True,
    )


def to_patches(frame_major, times_local):
    width = frame_major.shape[-1]
    grouped = frame_major.reshape(times_local, -1, width)
    moved = lax.all_to_all(grouped, "dp", split_axis=1, concat_axis=0, tiled=True)
    return moved.reshape(TIMES, -1, width)


def to_frames(patch_major, times_local):
    width = patch_major.shape[-1]
    grouped = patch_major.reshape(lax.axis_size("dp") * times_local, -1, width)
    moved = lax.all_to_all(grouped, "dp", split_axis=0, concat_axis=1, tiled=True)
    return moved.reshape(-1, width)


def in_weights(inproj, bias_pair):
    width = inproj.shape[2]
    weight = inproj.reshape(inproj.shape[0], 3 * width)
    zero_part = jnp.zeros((width,), jnp.float32)
    bias = jnp.concatenate(
        [bias_pair[0].astype(jnp.float32), zero_part, bias_pair[1].astype(jnp.float32)]
    )
    return (weight, bias)


def attention_forward(resid, gain, shift, weight_set, outbias, temporal, times_local):
    inproj, bias_pair, outproj = weight_set
    normed, norm_pull = jax.vjp(layer_norm, resid, gain, shift)
    rows_in = full_rows(normed.astype(jnp.bfloat16))
    weight, bias = in_weights(inproj, bias_pair)
    width = inproj.shape[2]
    projected = (jnp.dot(rows_in, weight, preferred_element_type=jnp.float32) + bias).astype(
        jnp.bfloat16
    )
    heads_here = projected.shape[-1] // (3 * HS)
    if temporal:
        projected = to_patches(projected, times_local)
        split_heads = projected.reshape(TIMES, -1, 3, heads_here, HS)
    else:
        split_heads = projected.reshape(-1, PATCH, 3, heads_here, HS)
    mixed, log_total = attend(
        split_heads[:, :, 0], split_heads[:, :, 1], split_heads[:, :, 2], not temporal
    )
    if temporal:
        mixed_low = to_frames(
            mixed.astype(jnp.bfloat16).reshape(TIMES, -1, heads_here * HS), times_local
        )
    else:
        mixed_low = mixed.astype(jnp.bfloat16).reshape(-1, width)

    def out_term(start, count):
        return jnp.dot(
            lax.dynamic_slice_in_dim(mixed_low, start, count, 0),
            outproj,
            preferred_element_type=jnp.float32,
        )

    branch = partial_rows(out_term, resid.shape[0]) + outbias.astype(jnp.float32)
    kept = (norm_pull, rows_in, split_heads, log_total, mixed_low)
    return (resid + branch, kept)


def attention_backward(upstream, kept, weight_set, temporal, times_local):
    inproj, bias_pair, outproj = weight_set
    norm_pull, rows_in, split_heads, log_total, mixed_low = kept
    contract_rows = (((0,), (0,)), ((), ()))
    contract_cols = (((1,), (1,)), ((), ()))
    branch_low = upstream.astype(jnp.bfloat16)
    outbias_grad = jnp.sum(branch_low, axis=0, dtype=jnp.float32)
    branch_rows = full_rows(branch_low)
    outproj_grad = lax.dot_general(
        mixed_low, branch_rows, contract_rows, preferred_element_type=jnp.float32
    )
    mixed_grad = lax.dot_general(
        branch_rows, outproj, contract_cols, preferred_element_type=jnp.float32
    ).astype(jnp.bfloat16)
    width = inproj.shape[2]
    heads_here = split_heads.shape[3]
    if temporal:
        mixed_grad = to_patches(mixed_grad, times_local)
    mixed_grad = mixed_grad.reshape(split_heads.shape[0], split_heads.shape[1], heads_here, HS)
    query_grad, key_grad, value_grad = attend_back(
        split_heads[:, :, 0],
        split_heads[:, :, 1],
        split_heads[:, :, 2],
        log_total,
        mixed_grad,
        not temporal,
    )
    projected_grad = jnp.stack([query_grad, key_grad, value_grad], axis=2).astype(jnp.bfloat16)
    if temporal:
        projected_grad = to_frames(
            projected_grad.reshape(TIMES, -1, 3 * heads_here * HS), times_local
        )
    else:
        projected_grad = projected_grad.reshape(-1, 3 * width)
    column_sums = jnp.sum(projected_grad, axis=0, dtype=jnp.float32).reshape(3, width)
    bias_grad = jnp.stack([column_sums[0], column_sums[2]])
    weight = inproj.reshape(inproj.shape[0], 3 * width)
    inproj_grad = lax.dot_general(
        rows_in, projected_grad, contract_rows, preferred_element_type=jnp.float32
    ).reshape(inproj.shape)

    def in_term(start, count):
        return lax.dot_general(
            lax.dynamic_slice_in_dim(projected_grad, start, count, 0),
            weight,
            contract_cols,
            preferred_element_type=jnp.float32,
        )

    normed_grad = partial_rows(in_term, upstream.shape[0])
    resid_grad, gain_grad, shift_grad = norm_pull(normed_grad)
    return (
        upstream + resid_grad,
        (gain_grad, shift_grad, inproj_grad, bias_grad, outproj_grad, outbias_grad),
    )


def per_device(
    tokens,
    space_gain,
    space_shift,
    space_inproj,
    space_bias,
    space_outproj,
    space_outbias,
    time_gain,
    time_shift,
    time_inproj,
    time_bias,
    time_outproj,
    time_outbias,
    feed_gain,
    feed_shift,
    up_weight,
    up_bias,
    down_weight,
    down_bias,
    cotangent,
):
    clips_local = min(TIMES, lax.axis_size("dp"))
    times_local = TIMES // clips_local
    own_rows = tokens.shape[0] * tokens.shape[1]
    contract_rows = (((0,), (0,)), ((), ()))
    contract_cols = (((1,), (1,)), ((), ()))
    time_set = (time_inproj, time_bias, time_outproj)
    space_set = (space_inproj, space_bias, space_outproj)
    resid = tokens.reshape(own_rows, -1).astype(jnp.float32)
    after_space, space_kept = attention_forward(
        resid, space_gain, space_shift, space_set, space_outbias, False, times_local
    )
    after_time, time_kept = attention_forward(
        after_space, time_gain, time_shift, time_set, time_outbias, True, times_local
    )
    feed_normed, feed_pull = jax.vjp(layer_norm, after_time, feed_gain, feed_shift)
    feed_low = feed_normed.astype(jnp.bfloat16)
    branch_low = cotangent.reshape(own_rows, -1)
    upstream = branch_low.astype(jnp.float32)
    down_bias_grad = jnp.sum(branch_low, axis=0, dtype=jnp.float32)
    feed_full = full_rows(feed_low)
    pre_act = lax.dot_general(
        feed_full, up_weight, contract_cols, preferred_element_type=jnp.float32
    ) + up_bias.astype(jnp.float32)
    hidden = gelu_exact(pre_act).astype(jnp.bfloat16)

    def down_term(start, count):
        return jnp.dot(hidden, down_weight, preferred_element_type=jnp.float32)

    layer_sum = after_time + partial_rows(down_term, own_rows) + down_bias.astype(jnp.float32)
    branch_full = full_rows(branch_low)
    down_grad = lax.dot_general(
        hidden, branch_full, contract_rows, preferred_element_type=jnp.float32
    )
    hidden_grad = lax.dot_general(
        branch_full, down_weight, contract_cols, preferred_element_type=jnp.float32
    )
    pre_grad = (hidden_grad * gelu_slope(pre_act)).astype(jnp.bfloat16)
    up_grad = lax.dot_general(
        pre_grad, feed_full, contract_rows, preferred_element_type=jnp.float32
    )
    up_bias_grad = jnp.sum(pre_grad, axis=0, dtype=jnp.float32)

    def up_term(start, count):
        return jnp.dot(pre_grad, up_weight, preferred_element_type=jnp.float32)

    feed_grad = partial_rows(up_term, own_rows)
    resid_part, feed_gain_grad, feed_shift_grad = feed_pull(feed_grad)
    time_upstream = upstream + resid_part
    space_upstream, time_grads = attention_backward(
        time_upstream, time_kept, time_set, True, times_local
    )
    input_grad, space_grads = attention_backward(
        space_upstream, space_kept, space_set, False, times_local
    )
    summed = lax.psum(
        (
            space_grads[2],
            space_grads[3],
            space_grads[4],
            time_grads[2],
            time_grads[3],
            time_grads[4],
            up_grad,
            up_bias_grad,
            down_grad,
        ),
        "dp",
    )
    shared = lax.psum(
        (
            space_grads[0],
            space_grads[1],
            space_grads[5],
            time_grads[0],
            time_grads[1],
            time_grads[5],
            feed_gain_grad,
            feed_shift_grad,
            down_bias_grad,
        ),
        ("dp", "tensor"),
    )
    shape_out = tokens.shape
    return (
        layer_sum.astype(jnp.bfloat16).reshape(shape_out),
        input_grad.reshape(shape_out),
        shared[0],
        shared[1],
        summed[0],
        summed[1],
        summed[2],
        shared[2],
        shared[3],
        shared[4],
        summed[3],
        summed[4],
        summed[5],
        shared[5],
        shared[6],
        shared[7],
        summed[6],
        summed[7],
        summed[8],
        shared[8],
    )


def solution(mesh):
    return jax.shard_map(
        per_device,
        mesh=mesh,
        in_specs=(
            P(("dp", "tensor"), None, None),
            P(),
            P(),
            P(None, None, "tensor"),
            P(None, "tensor"),
            P("tensor", None),
            P(),
            P(),
            P(),
            P(None, None, "tensor"),
            P(None, "tensor"),
            P("tensor", None),
            P(),
            P(),
            P(),
            P("tensor", None),
            P("tensor"),
            P("tensor", None),
            P(),
            P(("dp", "tensor"), None, None),
        ),
        out_specs=(
            P(("dp", "tensor"), None, None),
            P(("dp", "tensor"), None, None),
            P(),
            P(),
            P(None, None, "tensor"),
            P(None, "tensor"),
            P("tensor", None),
            P(),
            P(),
            P(),
            P(None, None, "tensor"),
            P(None, "tensor"),
            P("tensor", None),
            P(),
            P(),
            P(),
            P("tensor", None),
            P("tensor"),
            P("tensor", None),
            P(),
        ),
        check_vma=False,
    )
```

profile of v0, /device:TPU:0, one launch (start us, length us, event | category | flops | bytes accessed | tf_op | source)
XLA Modules:
  0.0 2199.9 jit_solution(4943705803411020907)
XLA Ops:
  19.9 93.2 %all-gather.7.cloned.1.call-done = bf16[3136,768]{1,0:T(8,128)(2,1)} async-done(((bf16[784,768]{1,0:T(8,128)(2,1)}), bf16[3136,768]{1,0:T(8,128)(2,1)}) %all-gather.7.cloned.1.call-update) | async-done | bytes 4816912 | tf_op jit(solution)/shard_map/all_gather | solution.py:99
  113.1 7.1 add_convert_fusion.1
  120.2 15.5 reshape.274
  154.1 5.1 fusion.76
  160.0 162.2 %reduce-scatter.7.cloned.1.call-done = f32[784,768]{1,0:T(8,128)} async-done(((f32[3136,768]{1,0:T(8,128)}), f32[784,768]{1,0:T(8,128)}) %reduce-scatter.7.cloned.1.call-update) | async-done | bytes 2408464 | tf_op jit(solution)/shard_map/reduce_scatter | solution.py:103
  328.0 92.1 %all-gather.9.cloned.1.call-done = bf16[3136,768]{1,0:T(8,128)(2,1)} async-done(((bf16[784,768]{1,0:T(8,128)(2,1)}), bf16[3136,768]{1,0:T(8,128)(2,1)}) %all-gather.9.cloned.1.call-update) | async-done | bytes 4816912 | tf_op jit(solution)/shard_map/all_gather | solution.py:99
  420.1 7.1 add_convert_fusion
  427.1 9.2 reshape.277
  436.3 16.3 copy.164
  452.6 51.6 %all_to_all.60 = bf16[2,1568,576]{2,0,1:T(2,128)(2,1)} all-to-all(bf16[2,1568,576]{2,0,1:T(2,128)(2,1)} %copy.164), channel_id=1, replica_groups=mesh['dp'=8,'tensor'=4] {'dp'}, dimensions={1} | all-to-all | bytes 7225344 | tf_op jit(solution)/shard_map/all_to_all | solution.py:114
  504.2 13.3 copy.199
  548.7 23.4 %all_to_all.61 = bf16[16,196,192]{1,2,0:T(8,128)(2,1)S(1)} all-to-all(bf16[16,196,192]{1,2,0:T(8,128)(2,1)S(1)} %bitcast.180), channel_id=1, replica_groups=mesh['dp'=8,'tensor'=4] {'dp'}, dimensions={0} | all-to-all | bytes 2408448 | tf_op jit(solution)/shard_map/all_to_all | solution.py:121
  583.4 160.4 %reduce-scatter.9.cloned.1.call-done = f32[784,768]{1,0:T(8,128)} async-done(((f32[3136,768]{1,0:T(8,128)}), f32[784,768]{1,0:T(8,128)}) %reduce-scatter.9.cloned.1.call-update) | async-done | bytes 2408464 | tf_op jit(solution)/shard_map/reduce_scatter | solution.py:103
  752.2 89.5 %all-gather.11.cloned.1.call-done = bf16[3136,768]{1,0:T(8,128)(2,1)} async-done(((bf16[784,768]{1,0:T(8,128)(2,1)}), bf16[3136,768]{1,0:T(8,128)(2,1)}) %all-gather.11.cloned.1.call-update) | async-done | bytes 4816912 | tf_op jit(solution)/shard_map/all_gather | solution.py:99
  841.7 9.5 multiply_convert_fusion.1
  851.2 81.9 %all-gather.13.cloned.1.call-done = bf16[3136,768]{1,0:T(8,128)(2,1)} async-done(((bf16[784,768]{1,0:T(8,128)(2,1)}), bf16[3136,768]{1,0:T(8,128)(2,1)}) %all-gather.13.cloned.1.call-update) | async-done | bytes 4816912 | tf_op jit(solution)/shard_map/all_gather | solution.py:99
  933.1 9.9 convert_reduce_fusion
  945.1 6.3 fusion.79
  951.5 8.8 fusion.78
  961.0 153.3 %reduce-scatter.13.cloned.1.call-done = f32[784,768]{1,0:T(8,128)} async-done(((f32[3136,768]{1,0:T(8,128)}), f32[784,768]{1,0:T(8,128)}) %reduce-scatter.13.cloned.1.call-update) | async-done | bytes 2408464 | tf_op jit(solution)/shard_map/reduce_scatter | solution.py:103
  1117.7 164.4 %reduce-scatter.11.cloned.1.call-done = f32[784,768]{1,0:T(8,128)} async-done(((f32[3136,768]{1,0:T(8,128)}), f32[784,768]{1,0:T(8,128)}) %reduce-scatter.11.cloned.1.call-update) | async-done | bytes 2408464 | tf_op jit(solution)/shard_map/reduce_scatter | solution.py:103
  1282.0 5.2 fusion.69
  1289.1 92.2 %all-gather.15.cloned.1.call-done = bf16[3136,768]{1,0:T(8,128)(2,1)} async-done(((bf16[784,768]{1,0:T(8,128)(2,1)}), bf16[3136,768]{1,0:T(8,128)(2,1)}) %all-gather.15.cloned.1.call-update) | async-done | bytes 4816912 | tf_op jit(solution)/shard_map/all_gather | solution.py:99
  1390.4 7.2 copy.174
  1402.1 21.2 all-to-all-done.2
  1423.2 6.0 copy.201
  1450.5 10.7 copy.180
  1461.2 7.4 copy.181
  1468.6 51.8 %all_to_all.62 = bf16[16,196,576]{2,1,0:T(8,128)(2,1)S(1)} all-to-all(bf16[16,196,576]{2,1,0:T(8,128)(2,1)} %copy.181), channel_id=1, replica_groups=mesh['dp'=8,'tensor'=4] {'dp'}, dimensions={0} | all-to-all | bytes 7225344 | tf_op jit(solution)/shard_map/all_to_all | solution.py:121
  1524.7 5.4 reshape.285
  1530.1 10.0 fusion.80
  1540.1 161.0 %reduce-scatter.15.cloned.1.call-done = f32[784,768]{1,0:T(8,128)} async-done(((f32[3136,768]{1,0:T(8,128)}), f32[784,768]{1,0:T(8,128)}) %reduce-scatter.15.cloned.1.call-update) | async-done | bytes 2408464 | tf_op jit(solution)/shard_map/reduce_scatter | solution.py:103
  1709.3 92.1 %all-gather.17.cloned.1.call-done = bf16[3136,768]{1,0:T(8,128)(2,1)} async-done(((bf16[784,768]{1,0:T(8,128)(2,1)}), bf16[3136,768]{1,0:T(8,128)(2,1)}) %all-gather.17.cloned.1.call-update) | async-done | bytes 4816912 | tf_op jit(solution)/shard_map/all_gather | solution.py:99
  1806.5 7.1 reshape.286
  1813.6 7.8 fusion.46
  1821.4 8.8 multiply_reduce_fusion
  1830.2 11.1 multiply_convert_fusion
  1854.0 10.0 convert_element_type.196
  1863.9 9.9 fusion.81
  1874.2 9.6 fusion.85
  1883.8 9.6 fusion.84
  1895.4 6.5 copy.189
  1901.8 7.9 fusion.13
  1914.3 6.7 fusion.15
  1931.0 15.5 all-reduce.1
  1946.5 90.2 %reduce-scatter.17.cloned.1.call-done = f32[784,768]{1,0:T(8,128)} async-done(((f32[3136,768]{1,0:T(8,128)}), f32[784,768]{1,0:T(8,128)}) %reduce-scatter.17.cloned.1.call-update) | async-done | bytes 2408464 | tf_op jit(solution)/shard_map/reduce_scatter | solution.py:103
  2052.2 43.8 %all-reduce = (f32[768]{0:T(1024)}, f32[768]{0:T(1024)}, f32[768]{0:T(1024)}, f32[768]{0:T(1024)}, f32[768]{0:T(1024)}, /*index=5*/f32[768]{0:T(1024)}, f32[768]{0:T(1024)}, f32[768]{0:T(1024)}, f32[768]{0:T(1024)}) all-reduce(f32[768]{0:T(1024)S(1)} %get-tuple-element.124, ...), channel_id=1, replica_groups=mesh['dp'=8,'tensor'=4] {'dp','tensor'}, use_global_device_ids=true, to_apply=%region_25.0 | all-reduce | flops 6912 | bytes 55296 | tf_op jit(solution)/shard_map/psum | solution.py:319
  2096.0 86.8 %all-reduce.5.cloned.1.call-done = (f32[768,3,192]{0,2,1:T(8,128)}, f32[192,768]{1,0:T(8,128)}, f32[768,3,192]{0,2,1:T(8,128)}, f32[192,768]{1,0:T(8,128)}, f32[768,768]{1,0:T(8,128)}, /*index=5*/f32[768,768]{1,0:T(8,128)}) async-done(((f32[768,3,192]{0,2,1:T(8,128)}, f32[192,768]{1,0:T(8,128)}, f32[768,3,192]{0,2,1:T(8,128)}, f32[192,768]{1,0:T(8,128)}, f32[768,768]{1,0:T(8,128)}, ...) | async-done | bytes 9437200 | tf_op jit(solution)/shard_map/psum | solution.py:305
  (288 shorter events, 203.8 us)
Async XLA Ops:
  7.2 834.5 %copy-start = (bf16[768,768]{1,0:T(8,128)(2,1)S(1)}, bf16[768,768]{1,0:T(8,128)(2,1)}, u32[]{:S(2)}) copy-start(bf16[768,768]{1,0:T(8,128)(2,1)} %param.35) | copy-start | bytes 3538948
  7.2 105.9 %all-gather.7.cloned.1.call-start = ((), (), s32[]{:S(2)}) async-start(), calls=%async_computation.10 | async-start | bytes 6021120 | tf_op jit(solution)/shard_map/all_gather | solution.py:99
  15.9 3.9 copy-start.67
  15.9 97.2 %copy-start.74 = (bf16[768,3,192]{0,2,1:T(8,128)(2,1)S(1)}, bf16[768,3,192]{0,2,1:T(8,128)(2,1)}, u32[]{:S(2)}) copy-start(bf16[768,3,192]{0,2,1:T(8,128)(2,1)} %param.23) | copy-start | bytes 2654212
  19.2 303.0 %reduce-scatter.7.cloned.1.call-start = ((), (), s32[]{:S(2)}) async-start(), calls=%async_computation.11 | async-start | bytes 12042240 | tf_op jit(solution)/shard_map/reduce_scatter | solution.py:103
  138.3 5.5 copy-start.31
  143.8 4.6 copy-start.48
  148.5 5.7 copy-start.46
  154.1 5.2 copy-start.27
  159.3 260.8 %all-gather.9.cloned.1.call-start = ((), (), s32[]{:S(2)}) async-start(), calls=%async_computation.12 | async-start | bytes 6021120 | tf_op jit(solution)/shard_map/all_gather | solution.py:99
  326.4 93.7 %copy-start.73 = (bf16[768,3,192]{0,2,1:T(8,128)(2,1)S(1)}, bf16[768,3,192]{0,2,1:T(8,128)(2,1)}, u32[]{:S(2)}) copy-start(bf16[768,3,192]{0,2,1:T(8,128)(2,1)} %param.29) | copy-start | bytes 2654212
  327.9 415.9 %reduce-scatter.9.cloned.1.call-start = ((), (), s32[]{:S(2)}) async-start(), calls=%async_computation.13 | async-start | bytes 12042240 | tf_op jit(solution)/shard_map/reduce_scatter | solution.py:103
  572.1 5.5 copy-start.44
  577.5 5.2 copy-start.29
  582.7 259.0 %all-gather.11.cloned.1.call-start = ((), (), s32[]{:S(2)}) async-start(), calls=%async_computation.14 | async-start | bytes 6021120 | tf_op jit(solution)/shard_map/all_gather | solution.py:99
  749.5 183.6 %all-gather.13.cloned.1.call-start = ((), (), s32[]{:S(2)}) async-start(), calls=%async_computation.16 | async-start | bytes 6021120 | tf_op jit(solution)/shard_map/all_gather | solution.py:99
  752.1 362.2 %reduce-scatter.13.cloned.1.call-start = ((), (), s32[]{:S(2)}) async-start(), calls=%async_computation.17 | async-start | bytes 12042240 | tf_op jit(solution)/shard_map/reduce_scatter | solution.py:103
  752.2 180.9 %copy-start.72 = (bf16[768,768]{1,0:T(8,128)(2,1)S(1)}, bf16[768,768]{1,0:T(8,128)(2,1)}, u32[]{:S(2)}) copy-start(bf16[768,768]{1,0:T(8,128)(2,1)} %param.37) | copy-start | bytes 3538948
  951.5 330.6 %reduce-scatter.11.cloned.1.call-start = ((), (), s32[]{:S(2)}) async-start(), calls=%async_computation.15 | async-start | bytes 12042240 | tf_op jit(solution)/shard_map/reduce_scatter | solution.py:103
  960.3 420.9 %all-gather.15.cloned.1.call-start = ((), (), s32[]{:S(2)}) async-start(), calls=%async_computation.18 | async-start | bytes 6021120 | tf_op jit(solution)/shard_map/all_gather | solution.py:99
  1117.6 169.6 %copy-start.12 = (bf16[784,768]{1,0:T(8,128)(2,1)S(1)}, bf16[784,768]{1,0:T(8,128)(2,1)}, u32[]{:S(2)}) copy-start(bf16[784,768]{1,0:T(8,128)(2,1)} %reshape.282) | copy-start | bytes 3612676
  1287.2 94.0 %copy-start.45 = (bf16[192,768]{1,0:T(8,128)(2,1)S(1)}, bf16[192,768]{1,0:T(8,128)(2,1)}, u32[]{:S(2)}) copy-start(bf16[192,768]{1,0:T(8,128)(2,1)} %param.31) | copy-start | bytes 884740
  1390.4 11.5 copy-start.39
  1397.6 25.7 %all-to-all-start.2 = ((bf16[2,1568,192]{2,0,1:T(2,128)(2,1)}), bf16[2,1568,192]{2,0,1:T(2,128)(2,1)}, u32[]{:S(2)}, u32[]{:S(2)}) async-start(bf16[2,1568,192]{2,0,1:T(2,128)(2,1)} %copy.174), calls=%async_computation.6 | async-start | bytes 3211264 | tf_op jit(solution)/shard_map/all_to_all | solution.py:114
  1401.8 299.3 %reduce-scatter.15.cloned.1.call-start = ((), (), s32[]{:S(2)}) async-start(), calls=%async_computation.19 | async-start | bytes 12042240 | tf_op jit(solution)/shard_map/reduce_scatter | solution.py:103
  1429.2 9.5 slice-start
  1434.0 4.7 slice-start.1
  1434.0 5.1 copy-start.19
  1434.0 5.8 copy-start.26
  1540.1 164.5 %copy-start.59 = (f32[784]{0:T(1024)S(1)}, f32[784]{0:T(1024)}, u32[]{:S(2)}) copy-start(f32[784]{0:T(1024)} %copy-done.58) | copy-start | bytes 9412
  1540.1 261.3 %all-gather.17.cloned.1.call-start = ((), (), s32[]{:S(2)}) async-start(), calls=%async_computation.20 | async-start | bytes 6021120 | tf_op jit(solution)/shard_map/all_gather | solution.py:99
  1707.4 94.0 %copy-start.47 = (bf16[192,768]{1,0:T(8,128)(2,1)S(1)}, bf16[192,768]{1,0:T(8,128)(2,1)}, u32[]{:S(2)}) copy-start(bf16[192,768]{1,0:T(8,128)(2,1)} %param.25) | copy-start | bytes 884740
  1709.2 327.6 %reduce-scatter.17.cloned.1.call-start = ((), (), s32[]{:S(2)}) async-start(), calls=%async_computation.21 | async-start | bytes 12042240 | tf_op jit(solution)/shard_map/reduce_scatter | solution.py:103
  1813.6 7.8 copy-start.20
  1813.6 7.8 copy-start.32
  1841.2 4.5 copy-start.5
  1841.2 4.8 copy-start.14
  1873.9 308.9 %all-reduce.5.cloned.1.call-start = ((), (), s32[]{:S(2)}) async-start(), calls=%async_computation.22 | async-start | bytes 18874368 | tf_op jit(solution)/shard_map/psum | solution.py:305
  1874.2 19.2 slice-start.2
  1883.8 9.6 copy-start.30
  1883.8 9.6 slice-start.3
  1901.8 7.9 copy-start.28
  1909.8 4.6 copy-start.34
  1927.9 108.9 %copy-start.51 = (f32[784]{0:T(1024)S(1)}, f32[784]{0:T(1024)}, u32[]{:S(2)}) copy-start(f32[784]{0:T(1024)} %copy-done.50) | copy-start | bytes 9412
  1927.9 108.9 %copy-start.53 = (f32[784]{0:T(1024)S(1)}, f32[784]{0:T(1024)}, u32[]{:S(2)}) copy-start(f32[784]{0:T(1024)} %copy-done.52) | copy-start | bytes 9412
  1927.9 108.9 %copy-start.57 = (f32[768]{0:T(1024)S(1)}, f32[768]{0:T(1024)}, u32[]{:S(2)}) copy-start(f32[768]{0:T(1024)} %param.21) | copy-start | bytes 9220
  1946.5 93.8 %copy-start.61 = (f32[784]{0:T(1024)S(1)}, f32[784]{0:T(1024)}, u32[]{:S(2)}) copy-start(f32[784]{0:T(1024)} %copy-done.60) | copy-start | bytes 9412
  2189.1 3.9 copy-start.1
  (46 other events, 105.5 us)
Sparse Core Ops, SparseCore 0:
  19.3 93.7 all-gather.6
  159.4 162.6 reduce-scatter.6
  328.0 92.0 all-gather.8
  582.8 160.8 reduce-scatter.8
  749.6 92.0 all-gather.10
  843.7 89.3 all-gather.12
  951.6 162.6 reduce-scatter.12
  1116.7 165.3 reduce-scatter.10
  1289.2 92.0 all-gather.14
  1540.2 160.8 reduce-scatter.14
  1709.3 92.0 all-gather.16
  1874.0 162.6 reduce-scatter.16
  2043.0 139.7 all-reduce.4
where the time goes:
time: 2210 us; the launch traced here: 2200 us
  waiting for transfers between devices  1540 us (70%)
  local copies, waits for them, and re-layouts  211 us (10%)
  blocking collectives  186 us (8%)
  matrix products  174 us (8%)
  other arithmetic  67.5 us (3%)
    reduce_scatter x6, waiting for transfers between devices, partial_rows(): lax.psum_scatter(make_term(jnp.int32(0), own_rows * lax.axis_size('tensor...  891 us
    all_gather x6, waiting for transfers between devices, full_rows(): return lax.all_gather(shard, 'tensor', axis=0, tiled=True)  541 us
    psum x1, waiting for transfers between devices, per_device(): lax.psum((space_grads[2], space_grads[3], space_grads[4], time_grads[2],...  86.8 us
    all_to_all x2, blocking collectives, to_frames(): lax.all_to_all(grouped, 'dp', split_axis=0, concat_axis=1, tiled=True)  75.2 us
    all_to_all x1, blocking collectives, to_patches(): lax.all_to_all(grouped, 'dp', split_axis=1, concat_axis=0, tiled=True)  51.6 us
    unnamed x174, local copies, waits for them, and re-layouts  46.9 us
  transfers between devices with their start and end apart: 14, of which 14 were waited for; matrix products, arithmetic and copies ran while one was open for 4% of the time, Pallas kernels for 0%

commit v1 on v0

--- a/solution.py
+++ b/solution.py
@@ -9,6 +9,28 @@
 EPSILON = 1e-06
 ROOT_HALF = 0.7071067811865476
 INV_ROOT_TAU = 0.3989422804014327
+
+
+def in_order(blocks, dim):
+    blocks = jnp.moveaxis(blocks, 0, dim)
+    dims = blocks.shape
+    return blocks.reshape(*dims[:dim], dims[dim] * dims[dim + 1], *dims[dim + 2 :])
+
+
+def ring_gather(value, axis, dim):
+    peers = lax.axis_size(axis)
+    pairs = [(i, (i + 1) % peers) for i in range(peers)]
+    back = [(b, a) for a, b in pairs]
+    lower, upper = ([], [])
+    for lap in range(peers - 1):
+        if lap % 2 == 0:
+            lower.append(lax.ppermute(lower[-1] if lower else value, axis, pairs))
+        else:
+            upper.append(lax.ppermute(upper[-1] if upper else value, axis, back))
+    blocks = jnp.stack([*lower[::-1], value, *upper])
+    shift = lax.axis_index(axis) - len(lower)
+    blocks = blocks[(jnp.arange(peers) - shift) % peers]
+    return in_order(blocks, dim)
 
 
 def layer_norm(values, gain, shift):
@@ -96,7 +118,7 @@
 
 
 def full_rows(shard):
-    return lax.all_gather(shard, "tensor", axis=0, tiled=True)
+    return ring_gather(shard, "tensor", 0)
 
 
 def partial_rows(make_term, own_rows):

time: 2210 us -> 2190 us (level)
  waiting for transfers between devices: 1540 us -> 1340 us
  starting transfers between devices: 6.14 us -> 131 us
  local copies, waits for them, and re-layouts: 211 us -> 251 us
  other arithmetic: 67.5 us -> 92.4 us
    all_gather x6 -> x0, waiting for transfers between devices: 541 us -> none  [full_rows(): return lax.all_gather(shard, 'tensor', axis=0, tiled=True)]
    ppermute x0 -> x18, waiting for transfers between devices: none -> 314 us  [the longest x12 282 us: ring_gather(): lower.append(lax.ppermute(lower[-1] if lower else value, axis, pairs))]
    ppermute x0 -> x18, starting transfers between devices: none -> 127 us  [the longest x12 111 us: ring_gather(): lower.append(lax.ppermute(lower[-1] if lower else value, axis, pairs))]
    gather x0 -> x6, local copies, waits for them, and re-layouts: none -> 32.8 us  [ring_gather(): blocks = blocks[(jnp.arange(peers) - shift) % peers]]
    reduce_scatter x6, waiting for transfers between devices: 891 us -> 919 us  [partial_rows(): lax.psum_scatter(make_term(jnp.int32(0), own_rows * lax.axis_size('tensor...]
    another operation x0 -> x8, other arithmetic: none -> 26.1 us  [ring_gather(): blocks = jnp.stack([*lower[::-1], value, *upper])]
    unnamed x174 -> x200, local copies, waits for them, and re-layouts: 46.9 us -> 48.6 us
  transfers between devices with their start and end apart: 14 -> 26, of which waited for: 14 -> 24; matrix products, arithmetic and copies ran while one was open for 4% -> 5% of each run, Pallas kernels for 0% -> 0%
where the time goes in v1:
time: 2190 us; the launch traced here: 2180 us
  waiting for transfers between devices  1340 us (61%)
  local copies, waits for them, and re-layouts  251 us (11%)
  blocking collectives  185 us (8%)
  matrix products  168 us (8%)
  starting transfers between devices  131 us (6%)
  other arithmetic  92.4 us (4%)
    reduce_scatter x6, waiting for transfers between devices, partial_rows(): lax.psum_scatter(make_term(jnp.int32(0), own_rows * lax.axis_size('tensor...  919 us
    ppermute x12, waiting for transfers between devices, ring_gather(): lower.append(lax.ppermute(lower[-1] if lower else value, axis, pairs))  282 us
    ppermute x12, starting transfers between devices, ring_gather(): lower.append(lax.ppermute(lower[-1] if lower else value, axis, pairs))  111 us
    psum x1, waiting for transfers between devices, per_device(): lax.psum((space_grads[2], space_grads[3], space_grads[4], time_grads[2],...  86.7 us
    all_to_all x2, blocking collectives, to_frames(): lax.all_to_all(grouped, 'dp', split_axis=0, concat_axis=1, tiled=True)  75.2 us
    all_to_all x1, blocking collectives, to_patches(): lax.all_to_all(grouped, 'dp', split_axis=1, concat_axis=0, tiled=True)  51.8 us
    unnamed x200, local copies, waits for them, and re-layouts  48.6 us
  transfers between devices with their start and end apart: 26, of which 24 were waited for; matrix products, arithmetic and copies ran while one was open for 5% of the time, Pallas kernels for 0%

profile of v1, /device:TPU:0, one launch (start us, length us, event | category | flops | bytes accessed | tf_op | source)
XLA Modules:
  0.0 2183.6 jit_solution(6206216354318372349)
XLA Ops:
  23.2 27.4 %collective-permute-done = bf16[784,768]{1,0:T(8,128)(2,1)} collective-permute-done((bf16[784,768]{1,0:T(8,128)(2,1)S(1)}, bf16[784,768]{1,0:T(8,128)(2,1)}, u32[]{:S(2)}, u32[]{:S(2)}) %collective-permute-start) | collective-permute-done | bytes 1204256 | tf_op jit(solution)/shard_map/ppermute | solution.py:27
  56.4 18.8 collective-permute-done.2
  75.2 26.2 %collective-permute-done.1 = bf16[784,768]{1,0:T(8,128)(2,1)} collective-permute-done((bf16[784,768]{1,0:T(8,128)(2,1)}, bf16[784,768]{1,0:T(8,128)(2,1)}, u32[]{:S(2)}, u32[]{:S(2)}) %collective-permute-start.1) | collective-permute-done | bytes 1204256 | tf_op jit(solution)/shard_map/ppermute | solution.py:27
  119.2 15.5 reshape.447
  159.0 163.1 %reduce-scatter.7.cloned.1.call-done = f32[784,768]{1,0:T(8,128)} async-done(((f32[3136,768]{1,0:T(8,128)}), f32[784,768]{1,0:T(8,128)}) %reduce-scatter.7.cloned.1.call-update) | async-done | bytes 2408464 | tf_op jit(solution)/shard_map/reduce_scatter | solution.py:125
  330.0 27.4 %collective-permute-done.3 = bf16[784,768]{1,0:T(8,128)(2,1)S(1)} collective-permute-done((bf16[784,768]{1,0:T(8,128)(2,1)S(1)}, bf16[784,768]{1,0:T(8,128)(2,1)S(1)}, u32[]{:S(2)}, u32[]{:S(2)}) %collective-permute-start.3) | collective-permute-done | bytes 1204256 | tf_op jit(solution)/shard_map/ppermute | solution.py:27
  357.4 25.1 %collective-permute-start.4 = (bf16[784,768]{1,0:T(8,128)(2,1)S(1)}, bf16[784,768]{1,0:T(8,128)(2,1)S(1)}, u32[]{:S(2)}, u32[]{:S(2)}) collective-permute-start(bf16[784,768]{1,0:T(8,128)(2,1)S(1)} %collective-permute-done.3), channel_id=1, source_target_pairs={{0,1},{1,2},{2,3},{3,0},{4,5},{5,6},{6,7},{7,4},{8,9},{9,10},{10,1... | collective-permute-start | bytes 3612680 | tf_op jit(solution)/shard_map/ppermute | solution.py:27
  383.1 24.5 %collective-permute-done.4 = bf16[784,768]{1,0:T(8,128)(2,1)S(1)} collective-permute-done((bf16[784,768]{1,0:T(8,128)(2,1)S(1)}, bf16[784,768]{1,0:T(8,128)(2,1)S(1)}, u32[]{:S(2)}, u32[]{:S(2)}) %collective-permute-start.4) | collective-permute-done | bytes 1204256 | tf_op jit(solution)/shard_map/ppermute | solution.py:27
  422.7 9.2 reshape.451
  431.8 16.3 copy.173
  448.2 51.8 %all_to_all.60 = bf16[2,1568,576]{2,0,1:T(2,128)(2,1)} all-to-all(bf16[2,1568,576]{2,0,1:T(2,128)(2,1)} %copy.173), channel_id=1, replica_groups=mesh['dp'=8,'tensor'=4] {'dp'}, dimensions={1} | all-to-all | bytes 7225344 | tf_op jit(solution)/shard_map/all_to_all | solution.py:136
  500.0 13.3 copy.209
  544.5 23.4 %all_to_all.61 = bf16[16,196,192]{1,2,0:T(8,128)(2,1)S(1)} all-to-all(bf16[16,196,192]{1,2,0:T(8,128)(2,1)S(1)} %bitcast.212), channel_id=1, replica_groups=mesh['dp'=8,'tensor'=4] {'dp'}, dimensions={0} | all-to-all | bytes 2408448 | tf_op jit(solution)/shard_map/all_to_all | solution.py:143
  582.9 183.5 %reduce-scatter.9.cloned.1.call-done = f32[784,768]{1,0:T(8,128)} async-done(((f32[3136,768]{1,0:T(8,128)}), f32[784,768]{1,0:T(8,128)}) %reduce-scatter.9.cloned.1.call-update) | async-done | bytes 2408464 | tf_op jit(solution)/shard_map/reduce_scatter | solution.py:125
  779.0 23.9 %collective-permute-done.6 = bf16[784,768]{1,0:T(8,128)(2,1)} collective-permute-done((bf16[784,768]{1,0:T(8,128)(2,1)}, bf16[784,768]{1,0:T(8,128)(2,1)}, u32[]{:S(2)}, u32[]{:S(2)}) %collective-permute-start.6) | collective-permute-done | bytes 1204256 | tf_op jit(solution)/shard_map/ppermute | solution.py:27
  802.9 25.3 %collective-permute-start.7 = (bf16[784,768]{1,0:T(8,128)(2,1)}, bf16[784,768]{1,0:T(8,128)(2,1)}, u32[]{:S(2)}, u32[]{:S(2)}) collective-permute-start(bf16[784,768]{1,0:T(8,128)(2,1)} %collective-permute-done.6), channel_id=1, source_target_pairs={{0,1},{1,2},{2,3},{3,0},{4,5},{5,6},{6,7},{7,4},{8,9},{9,10},{10,1... | collective-permute-start | bytes 3612680 | tf_op jit(solution)/shard_map/ppermute | solution.py:27
  830.4 24.1 %collective-permute-done.10 = bf16[784,768]{1,0:T(8,128)(2,1)} collective-permute-done((bf16[784,768]{1,0:T(8,128)(2,1)}, bf16[784,768]{1,0:T(8,128)(2,1)}, u32[]{:S(2)}, u32[]{:S(2)}) %collective-permute-start.10) | collective-permute-done | bytes 1204256 | tf_op jit(solution)/shard_map/ppermute | solution.py:27
  867.7 12.5 collective-permute-done.8
  880.2 24.6 %collective-permute-done.7 = bf16[784,768]{1,0:T(8,128)(2,1)} collective-permute-done((bf16[784,768]{1,0:T(8,128)(2,1)}, bf16[784,768]{1,0:T(8,128)(2,1)}, u32[]{:S(2)}, u32[]{:S(2)}) %collective-permute-start.7) | collective-permute-done | bytes 1204256 | tf_op jit(solution)/shard_map/ppermute | solution.py:27
  915.5 8.1 multiply_convert_fusion.1
  923.6 7.8 convert_reduce_fusion
  941.2 8.7 fusion.76
  950.6 152.3 %reduce-scatter.13.cloned.1.call-done = f32[784,768]{1,0:T(8,128)} async-done(((f32[3136,768]{1,0:T(8,128)}), f32[784,768]{1,0:T(8,128)}) %reduce-scatter.13.cloned.1.call-update) | async-done | bytes 2408464 | tf_op jit(solution)/shard_map/reduce_scatter | solution.py:125
  1106.8 163.6 %reduce-scatter.11.cloned.1.call-done = f32[784,768]{1,0:T(8,128)} async-done(((f32[3136,768]{1,0:T(8,128)}), f32[784,768]{1,0:T(8,128)}) %reduce-scatter.11.cloned.1.call-update) | async-done | bytes 2408464 | tf_op jit(solution)/shard_map/reduce_scatter | solution.py:125
  1281.1 27.2 %collective-permute-done.12 = bf16[784,768]{1,0:T(8,128)(2,1)S(1)} collective-permute-done((bf16[784,768]{1,0:T(8,128)(2,1)S(1)}, bf16[784,768]{1,0:T(8,128)(2,1)S(1)}, u32[]{:S(2)}, u32[]{:S(2)}) %collective-permute-start.12) | collective-permute-done | bytes 1204256 | tf_op jit(solution)/shard_map/ppermute | solution.py:27
  1308.3 25.3 %collective-permute-start.13 = (bf16[784,768]{1,0:T(8,128)(2,1)S(1)}, bf16[784,768]{1,0:T(8,128)(2,1)S(1)}, u32[]{:S(2)}, u32[]{:S(2)}) collective-permute-start(bf16[784,768]{1,0:T(8,128)(2,1)S(1)} %collective-permute-done.12), channel_id=1, source_target_pairs={{0,1},{1,2},{2,3},{3,0},{4,5},{5,6},{6,7},{7,4},{8,9},{9,10},{10,1... | collective-permute-start | bytes 3612680 | tf_op jit(solution)/shard_map/ppermute | solution.py:27
  1334.0 24.5 %collective-permute-done.13 = bf16[784,768]{1,0:T(8,128)(2,1)S(1)} collective-permute-done((bf16[784,768]{1,0:T(8,128)(2,1)S(1)}, bf16[784,768]{1,0:T(8,128)(2,1)S(1)}, u32[]{:S(2)}, u32[]{:S(2)}) %collective-permute-start.13) | collective-permute-done | bytes 1204256 | tf_op jit(solution)/shard_map/ppermute | solution.py:27
  1387.1 21.2 all-to-all-done.2
  1435.4 10.7 copy.190
  1446.1 7.4 copy.191
  1453.6 51.8 %all_to_all.62 = bf16[16,196,576]{2,1,0:T(8,128)(2,1)S(1)} all-to-all(bf16[16,196,576]{2,1,0:T(8,128)(2,1)} %copy.191), channel_id=1, replica_groups=mesh['dp'=8,'tensor'=4] {'dp'}, dimensions={0} | all-to-all | bytes 7225344 | tf_op jit(solution)/shard_map/all_to_all | solution.py:143
  1515.0 10.0 fusion.78
  1525.1 162.0 %reduce-scatter.15.cloned.1.call-done = f32[784,768]{1,0:T(8,128)} async-done(((f32[3136,768]{1,0:T(8,128)}), f32[784,768]{1,0:T(8,128)}) %reduce-scatter.15.cloned.1.call-update) | async-done | bytes 2408464 | tf_op jit(solution)/shard_map/reduce_scatter | solution.py:125
  1698.6 27.4 %collective-permute-done.15 = bf16[784,768]{1,0:T(8,128)(2,1)S(1)} collective-permute-done((bf16[784,768]{1,0:T(8,128)(2,1)S(1)}, bf16[784,768]{1,0:T(8,128)(2,1)S(1)}, u32[]{:S(2)}, u32[]{:S(2)}) %collective-permute-start.15) | collective-permute-done | bytes 1204256 | tf_op jit(solution)/shard_map/ppermute | solution.py:27
  1726.0 25.5 %collective-permute-start.16 = (bf16[784,768]{1,0:T(8,128)(2,1)S(1)}, bf16[784,768]{1,0:T(8,128)(2,1)S(1)}, u32[]{:S(2)}, u32[]{:S(2)}) collective-permute-start(bf16[784,768]{1,0:T(8,128)(2,1)S(1)} %collective-permute-done.15), channel_id=1, source_target_pairs={{0,1},{1,2},{2,3},{3,0},{4,5},{5,6},{6,7},{7,4},{8,9},{9,10},{10,1... | collective-permute-start | bytes 3612680 | tf_op jit(solution)/shard_map/ppermute | solution.py:27
  1751.7 24.5 %collective-permute-done.16 = bf16[784,768]{1,0:T(8,128)(2,1)S(1)} collective-permute-done((bf16[784,768]{1,0:T(8,128)(2,1)S(1)}, bf16[784,768]{1,0:T(8,128)(2,1)S(1)}, u32[]{:S(2)}, u32[]{:S(2)}) %collective-permute-start.16) | collective-permute-done | bytes 1204256 | tf_op jit(solution)/shard_map/ppermute | solution.py:27
  1796.0 7.8 fusion.42
  1803.8 9.0 multiply_reduce_fusion
  1812.7 11.2 multiply_convert_fusion
  1836.4 10.2 convert_element_type.220
  1846.6 9.8 fusion.79
  1856.5 9.6 fusion.85
  1866.1 9.6 fusion.84
  1884.4 8.1 fusion.82
  1911.4 13.9 all-reduce.1
  1925.3 95.0 %reduce-scatter.17.cloned.1.call-done = f32[784,768]{1,0:T(8,128)} async-done(((f32[3136,768]{1,0:T(8,128)}), f32[784,768]{1,0:T(8,128)}) %reduce-scatter.17.cloned.1.call-update) | async-done | bytes 2408464 | tf_op jit(solution)/shard_map/reduce_scatter | solution.py:125
  2036.0 43.7 %all-reduce = (f32[768]{0:T(1024)}, f32[768]{0:T(1024)}, f32[768]{0:T(1024)}, f32[768]{0:T(1024)}, f32[768]{0:T(1024)}, /*index=5*/f32[768]{0:T(1024)}, f32[768]{0:T(1024)}, f32[768]{0:T(1024)}, f32[768]{0:T(1024)}) all-reduce(f32[768]{0:T(1024)S(1)} %get-tuple-element.124, ...), channel_id=1, replica_groups=mesh['dp'=8,'tensor'=4] {'dp','tensor'}, use_global_device_ids=true, to_apply=%region_25.26 | all-reduce | flops 6912 | bytes 55296 | tf_op jit(solution)/shard_map/psum | solution.py:341
  2079.7 86.7 %all-reduce.5.cloned.1.call-done = (f32[768,3,192]{0,2,1:T(8,128)}, f32[192,768]{1,0:T(8,128)}, f32[768,3,192]{0,2,1:T(8,128)}, f32[192,768]{1,0:T(8,128)}, f32[768,768]{1,0:T(8,128)}, /*index=5*/f32[768,768]{1,0:T(8,128)}) async-done(((f32[768,3,192]{0,2,1:T(8,128)}, f32[192,768]{1,0:T(8,128)}, f32[768,3,192]{0,2,1:T(8,128)}, f32[192,768]{1,0:T(8,128)}, f32[768,768]{1,0:T(8,128)}, ...) | async-done | bytes 9437200 | tf_op jit(solution)/shard_map/psum | solution.py:327
  (353 shorter events, 360.1 us)
Async XLA Ops:
  7.2 908.3 %copy-start = (bf16[768,768]{1,0:T(8,128)(2,1)S(1)}, bf16[768,768]{1,0:T(8,128)(2,1)}, u32[]{:S(2)}) copy-start(bf16[768,768]{1,0:T(8,128)(2,1)} %param.35) | copy-start | bytes 3538948
  7.2 314.9 %reduce-scatter.7.cloned.1.call-start = ((), (), s32[]{:S(2)}) async-start(), calls=%async_computation.10 | async-start | bytes 12042240 | tf_op jit(solution)/shard_map/reduce_scatter | solution.py:125
  12.2 42.0 %copy-start.52 = (f32[784]{0:T(1024)}, f32[784]{0:T(1024)S(1)}, u32[]{:S(2)}) copy-start(f32[784]{0:T(1024)S(1)} %div.73) | copy-start | bytes 9412
  13.0 41.2 %copy-start.54 = (f32[784]{0:T(1024)}, f32[784]{0:T(1024)S(1)}, u32[]{:S(2)}) copy-start(f32[784]{0:T(1024)S(1)} %rsqrt.30) | copy-start | bytes 9412
  18.0 32.6 %collective-permute-start = (bf16[784,768]{1,0:T(8,128)(2,1)S(1)}, bf16[784,768]{1,0:T(8,128)(2,1)}, u32[]{:S(2)}, u32[]{:S(2)}) collective-permute-start(bf16[784,768]{1,0:T(8,128)(2,1)S(1)} %add_convert_fusion.6), channel_id=1, source_target_pairs={{0,1},{1,2},{2,3},{3,0},{4,5},{5,6},{6,7},{7,4},{8,9},{9,10},{10,1... | collective-permute-start | bytes 3612680 | tf_op jit(solution)/shard_map/ppermute | solution.py:27
  21.1 54.1 %collective-permute-start.2 = (bf16[784,768]{1,0:T(8,128)(2,1)S(1)}, bf16[784,768]{1,0:T(8,128)(2,1)}, u32[]{:S(2)}, u32[]{:S(2)}) collective-permute-start(bf16[784,768]{1,0:T(8,128)(2,1)S(1)} %add_convert_fusion.6), channel_id=1, source_target_pairs={{1,0},{2,1},{3,2},{0,3},{5,4},{6,5},{7,6},{4,7},{9,8},{10,9},{11,1... | collective-permute-start | bytes 3612680 | tf_op jit(solution)/shard_map/ppermute | solution.py:29
  50.6 50.8 %collective-permute-start.1 = (bf16[784,768]{1,0:T(8,128)(2,1)}, bf16[784,768]{1,0:T(8,128)(2,1)}, u32[]{:S(2)}, u32[]{:S(2)}) collective-permute-start(bf16[784,768]{1,0:T(8,128)(2,1)} %collective-permute-done), channel_id=1, source_target_pairs={{0,1},{1,2},{2,3},{3,0},{4,5},{5,6},{6,7},{7,4},{8,9},{9,10},{10,1... | collective-permute-start | bytes 3612680 | tf_op jit(solution)/shard_map/ppermute | solution.py:27
  158.3 608.1 %reduce-scatter.9.cloned.1.call-start = ((), (), s32[]{:S(2)}) async-start(), calls=%async_computation.11 | async-start | bytes 12042240 | tf_op jit(solution)/shard_map/reduce_scatter | solution.py:125
  324.9 57.6 %copy-start.4 = (f32[784,768]{1,0:T(8,128)}, f32[784,768]{1,0:T(8,128)S(1)}, u32[]{:S(2)}) copy-start(f32[784,768]{1,0:T(8,128)S(1)} %get-tuple-element.162) | copy-start | bytes 7225348
  324.9 57.5 %copy-start.50 = (f32[784]{0:T(1024)}, f32[784]{0:T(1024)S(1)}, u32[]{:S(2)}) copy-start(f32[784]{0:T(1024)S(1)} %broadcast_multiply_fusion.2) | copy-start | bytes 9412
  325.4 57.5 %copy-start.63 = (f32[784]{0:T(1024)}, f32[784]{0:T(1024)S(1)}, u32[]{:S(2)}) copy-start(f32[784]{0:T(1024)S(1)} %multiply_reduce_fusion.11) | copy-start | bytes 9412
  325.6 57.3 %copy-start.56 = (f32[784]{0:T(1024)}, f32[784]{0:T(1024)S(1)}, u32[]{:S(2)}) copy-start(f32[784]{0:T(1024)S(1)} %fusion.54) | copy-start | bytes 9412
  326.1 31.3 %collective-permute-start.3 = (bf16[784,768]{1,0:T(8,128)(2,1)S(1)}, bf16[784,768]{1,0:T(8,128)(2,1)S(1)}, u32[]{:S(2)}, u32[]{:S(2)}) collective-permute-start(bf16[784,768]{1,0:T(8,128)(2,1)S(1)} %add_convert_fusion.4), channel_id=1, source_target_pairs={{0,1},{1,2},{2,3},{3,0},{4,5},{5,6},{6,7},{7,4},{8,9},{9,10},{10,1... | collective-permute-start | bytes 3612680 | tf_op jit(solution)/shard_map/ppermute | solution.py:27
  327.6 55.5 %collective-permute-start.5 = (bf16[784,768]{1,0:T(8,128)(2,1)S(1)}, bf16[784,768]{1,0:T(8,128)(2,1)S(1)}, u32[]{:S(2)}, u32[]{:S(2)}) collective-permute-start(bf16[784,768]{1,0:T(8,128)(2,1)S(1)} %add_convert_fusion.4), channel_id=1, source_target_pairs={{1,0},{2,1},{3,2},{0,3},{5,4},{6,5},{7,6},{4,7},{9,8},{10,9},{11,1... | collective-permute-start | bytes 3612680 | tf_op jit(solution)/shard_map/ppermute | solution.py:29
  357.4 50.2 %collective-permute-start.4 = (bf16[784,768]{1,0:T(8,128)(2,1)S(1)}, bf16[784,768]{1,0:T(8,128)(2,1)S(1)}, u32[]{:S(2)}, u32[]{:S(2)}) collective-permute-start(bf16[784,768]{1,0:T(8,128)(2,1)S(1)} %collective-permute-done.3), channel_id=1, source_target_pairs={{0,1},{1,2},{2,3},{3,0},{4,5},{5,6},{6,7},{7,4},{8,9},{9,10},{10,1... | collective-permute-start | bytes 3612680 | tf_op jit(solution)/shard_map/ppermute | solution.py:27
  578.6 524.3 %reduce-scatter.13.cloned.1.call-start = ((), (), s32[]{:S(2)}) async-start(), calls=%async_computation.13 | async-start | bytes 12042240 | tf_op jit(solution)/shard_map/reduce_scatter | solution.py:125
  582.4 192.8 %collective-permute-start.9 = (bf16[784,768]{1,0:T(8,128)(2,1)S(1)}, bf16[784,768]{1,0:T(8,128)(2,1)}, u32[]{:S(2)}, u32[]{:S(2)}) collective-permute-start(bf16[784,768]{1,0:T(8,128)(2,1)S(1)} %reshape.457), channel_id=1, source_target_pairs={{0,1},{1,2},{2,3},{3,0},{4,5},{5,6},{6,7},{7,4},{8,9},{9,10},{10,1... | collective-permute-start | bytes 3612680 | tf_op jit(solution)/shard_map/ppermute | solution.py:27
  769.9 60.5 %copy-start.78 = (bf16[768]{0:T(1024)(128)(2,1)S(1)}, bf16[768]{0:T(1024)(128)(2,1)}, u32[]{:S(2)}) copy-start(bf16[768]{0:T(1024)(128)(2,1)} %param.36) | copy-start | bytes 4612
  771.4 31.5 %collective-permute-start.6 = (bf16[784,768]{1,0:T(8,128)(2,1)}, bf16[784,768]{1,0:T(8,128)(2,1)}, u32[]{:S(2)}, u32[]{:S(2)}) collective-permute-start(bf16[784,768]{1,0:T(8,128)(2,1)} %add_convert_fusion.3), channel_id=1, source_target_pairs={{0,1},{1,2},{2,3},{3,0},{4,5},{5,6},{6,7},{7,4},{8,9},{9,10},{10,1... | collective-permute-start | bytes 3612680 | tf_op jit(solution)/shard_map/ppermute | solution.py:27
  772.9 57.6 %collective-permute-start.11 = (bf16[784,768]{1,0:T(8,128)(2,1)S(1)}, bf16[784,768]{1,0:T(8,128)(2,1)}, u32[]{:S(2)}, u32[]{:S(2)}) collective-permute-start(bf16[784,768]{1,0:T(8,128)(2,1)S(1)} %reshape.457), channel_id=1, source_target_pairs={{1,0},{2,1},{3,2},{0,3},{5,4},{6,5},{7,6},{4,7},{9,8},{10,9},{11,1... | collective-permute-start | bytes 3612680 | tf_op jit(solution)/shard_map/ppermute | solution.py:29
  775.2 79.4 %collective-permute-start.10 = (bf16[784,768]{1,0:T(8,128)(2,1)}, bf16[784,768]{1,0:T(8,128)(2,1)}, u32[]{:S(2)}, u32[]{:S(2)}) collective-permute-start(bf16[784,768]{1,0:T(8,128)(2,1)} %collective-permute-done.9), channel_id=1, source_target_pairs={{0,1},{1,2},{2,3},{3,0},{4,5},{5,6},{6,7},{7,4},{8,9},{9,10},{10,1... | collective-permute-start | bytes 3612680 | tf_op jit(solution)/shard_map/ppermute | solution.py:27
  775.2 105.0 %collective-permute-start.8 = (bf16[784,768]{1,0:T(8,128)(2,1)}, bf16[784,768]{1,0:T(8,128)(2,1)}, u32[]{:S(2)}, u32[]{:S(2)}) collective-permute-start(bf16[784,768]{1,0:T(8,128)(2,1)} %add_convert_fusion.3), channel_id=1, source_target_pairs={{1,0},{2,1},{3,2},{0,3},{5,4},{6,5},{7,6},{4,7},{9,8},{10,9},{11,1... | collective-permute-start | bytes 3612680 | tf_op jit(solution)/shard_map/ppermute | solution.py:29
  802.9 101.9 %collective-permute-start.7 = (bf16[784,768]{1,0:T(8,128)(2,1)}, bf16[784,768]{1,0:T(8,128)(2,1)}, u32[]{:S(2)}, u32[]{:S(2)}) collective-permute-start(bf16[784,768]{1,0:T(8,128)(2,1)} %collective-permute-done.6), channel_id=1, source_target_pairs={{0,1},{1,2},{2,3},{3,0},{4,5},{5,6},{6,7},{7,4},{8,9},{9,10},{10,1... | collective-permute-start | bytes 3612680 | tf_op jit(solution)/shard_map/ppermute | solution.py:27
  909.9 13.7 slice-start.4
  939.9 330.6 %reduce-scatter.11.cloned.1.call-start = ((), (), s32[]{:S(2)}) async-start(), calls=%async_computation.12 | async-start | bytes 12042240 | tf_op jit(solution)/shard_map/reduce_scatter | solution.py:125
  1277.0 31.2 %collective-permute-start.12 = (bf16[784,768]{1,0:T(8,128)(2,1)S(1)}, bf16[784,768]{1,0:T(8,128)(2,1)S(1)}, u32[]{:S(2)}, u32[]{:S(2)}) collective-permute-start(bf16[784,768]{1,0:T(8,128)(2,1)S(1)} %get-tuple-element.150), channel_id=1, source_target_pairs={{0,1},{1,2},{2,3},{3,0},{4,5},{5,6},{6,7},{7,4},{8,9},{9,10},{10,1... | collective-permute-start | bytes 3612680 | tf_op jit(solution)/shard_map/ppermute | solution.py:27
  1278.5 55.4 %collective-permute-start.14 = (bf16[784,768]{1,0:T(8,128)(2,1)S(1)}, bf16[784,768]{1,0:T(8,128)(2,1)S(1)}, u32[]{:S(2)}, u32[]{:S(2)}) collective-permute-start(bf16[784,768]{1,0:T(8,128)(2,1)S(1)} %get-tuple-element.150), channel_id=1, source_target_pairs={{1,0},{2,1},{3,2},{0,3},{5,4},{6,5},{7,6},{4,7},{9,8},{10,9},{11,1... | collective-permute-start | bytes 3612680 | tf_op jit(solution)/shard_map/ppermute | solution.py:29
  1308.3 50.2 %collective-permute-start.13 = (bf16[784,768]{1,0:T(8,128)(2,1)S(1)}, bf16[784,768]{1,0:T(8,128)(2,1)S(1)}, u32[]{:S(2)}, u32[]{:S(2)}) collective-permute-start(bf16[784,768]{1,0:T(8,128)(2,1)S(1)} %collective-permute-done.12), channel_id=1, source_target_pairs={{0,1},{1,2},{2,3},{3,0},{4,5},{5,6},{6,7},{7,4},{8,9},{9,10},{10,1... | collective-permute-start | bytes 3612680 | tf_op jit(solution)/shard_map/ppermute | solution.py:27
  1382.6 25.7 %all-to-all-start.2 = ((bf16[2,1568,192]{2,0,1:T(2,128)(2,1)}), bf16[2,1568,192]{2,0,1:T(2,128)(2,1)}, u32[]{:S(2)}, u32[]{:S(2)}) async-start(bf16[2,1568,192]{2,0,1:T(2,128)(2,1)} %copy.184), calls=%async_computation.6 | async-start | bytes 3211264 | tf_op jit(solution)/shard_map/all_to_all | solution.py:136
  1386.9 300.2 %reduce-scatter.15.cloned.1.call-start = ((), (), s32[]{:S(2)}) async-start(), calls=%async_computation.14 | async-start | bytes 12042240 | tf_op jit(solution)/shard_map/reduce_scatter | solution.py:125
  1525.0 162.1 %copy-start.51 = (f32[784]{0:T(1024)S(1)}, f32[784]{0:T(1024)}, u32[]{:S(2)}) copy-start(f32[784]{0:T(1024)} %copy-done.50) | copy-start | bytes 9412
  1525.0 162.1 %copy-start.57 = (f32[784]{0:T(1024)S(1)}, f32[784]{0:T(1024)}, u32[]{:S(2)}) copy-start(f32[784]{0:T(1024)} %copy-done.56) | copy-start | bytes 9412
  1525.0 162.1 %copy-start.60 = (f32[768]{0:T(1024)S(1)}, f32[768]{0:T(1024)}, u32[]{:S(2)}) copy-start(f32[768]{0:T(1024)} %param.27) | copy-start | bytes 9220
  1525.0 165.5 %copy-start.64 = (f32[784]{0:T(1024)S(1)}, f32[784]{0:T(1024)}, u32[]{:S(2)}) copy-start(f32[784]{0:T(1024)} %copy-done.63) | copy-start | bytes 9412
  1525.0 495.3 %reduce-scatter.17.cloned.1.call-start = ((), (), s32[]{:S(2)}) async-start(), calls=%async_computation.15 | async-start | bytes 12042240 | tf_op jit(solution)/shard_map/reduce_scatter | solution.py:125
  1693.3 58.2 %copy-start.41 = (f32[16,3,196]{2,1,0:T(4,128)S(1)}, f32[16,3,196]{2,1,0:T(4,128)}, u32[]{:S(2)}) copy-start(f32[16,3,196]{2,1,0:T(4,128)} %copy-done.40) | copy-start | bytes 112900
  1693.4 58.2 %copy-start.49 = (f32[16,3,196]{2,1,0:T(4,128)S(1)}, f32[16,3,196]{2,1,0:T(4,128)}, u32[]{:S(2)}) copy-start(f32[16,3,196]{2,1,0:T(4,128)} %copy-done.48) | copy-start | bytes 112900
  1694.8 31.2 %collective-permute-start.15 = (bf16[784,768]{1,0:T(8,128)(2,1)S(1)}, bf16[784,768]{1,0:T(8,128)(2,1)S(1)}, u32[]{:S(2)}, u32[]{:S(2)}) collective-permute-start(bf16[784,768]{1,0:T(8,128)(2,1)S(1)} %get-tuple-element.152), channel_id=1, source_target_pairs={{0,1},{1,2},{2,3},{3,0},{4,5},{5,6},{6,7},{7,4},{8,9},{9,10},{10,1... | collective-permute-start | bytes 3612680 | tf_op jit(solution)/shard_map/ppermute | solution.py:27
  1696.3 55.4 %collective-permute-start.17 = (bf16[784,768]{1,0:T(8,128)(2,1)S(1)}, bf16[784,768]{1,0:T(8,128)(2,1)S(1)}, u32[]{:S(2)}, u32[]{:S(2)}) collective-permute-start(bf16[784,768]{1,0:T(8,128)(2,1)S(1)} %get-tuple-element.152), channel_id=1, source_target_pairs={{1,0},{2,1},{3,2},{0,3},{5,4},{6,5},{7,6},{4,7},{9,8},{10,9},{11,1... | collective-permute-start | bytes 3612680 | tf_op jit(solution)/shard_map/ppermute | solution.py:29
  1726.0 50.2 %collective-permute-start.16 = (bf16[784,768]{1,0:T(8,128)(2,1)S(1)}, bf16[784,768]{1,0:T(8,128)(2,1)S(1)}, u32[]{:S(2)}, u32[]{:S(2)}) collective-permute-start(bf16[784,768]{1,0:T(8,128)(2,1)S(1)} %collective-permute-done.15), channel_id=1, source_target_pairs={{0,1},{1,2},{2,3},{3,0},{4,5},{5,6},{6,7},{7,4},{8,9},{9,10},{10,1... | collective-permute-start | bytes 3612680 | tf_op jit(solution)/shard_map/ppermute | solution.py:27
  1856.4 309.9 %all-reduce.5.cloned.1.call-start = ((), (), s32[]{:S(2)}) async-start(), calls=%async_computation.16 | async-start | bytes 18874368 | tf_op jit(solution)/shard_map/psum | solution.py:327
  1856.5 19.2 slice-start.6
  1877.7 19.2 slice-start.2
  1884.4 12.6 slice-start.3
  1908.2 112.1 %copy-start.53 = (f32[784]{0:T(1024)S(1)}, f32[784]{0:T(1024)}, u32[]{:S(2)}) copy-start(f32[784]{0:T(1024)} %copy-done.52) | copy-start | bytes 9412
  1908.3 112.1 %copy-start.55 = (f32[784]{0:T(1024)S(1)}, f32[784]{0:T(1024)}, u32[]{:S(2)}) copy-start(f32[784]{0:T(1024)} %copy-done.54) | copy-start | bytes 9412
  1908.3 112.1 %copy-start.62 = (f32[768]{0:T(1024)S(1)}, f32[768]{0:T(1024)}, u32[]{:S(2)}) copy-start(f32[768]{0:T(1024)} %param.21) | copy-start | bytes 9220
  1925.3 98.5 %copy-start.66 = (f32[784]{0:T(1024)S(1)}, f32[784]{0:T(1024)}, u32[]{:S(2)}) copy-start(f32[784]{0:T(1024)} %copy-done.65) | copy-start | bytes 9412
  (71 other events, 275.2 us)
Sparse Core Ops, SparseCore 0:
  158.4 163.6 reduce-scatter.6
  578.7 187.6 reduce-scatter.8
  940.0 162.8 reduce-scatter.12
  1105.1 165.2 reduce-scatter.10
  1525.2 161.8 reduce-scatter.14
  1856.6 163.6 reduce-scatter.16
  2026.5 139.7 all-reduce.4
